TPU v7x, 32 devices: a whole 2x2x4 slice. The times are simulated.
32 devices in a mesh: gx: 2 (over y), gy: 4 (over x, core), gz: 4 (over z).
Axes of the slice: x: 2, y: 2, z: 4, core: 2. Of those that a mesh axis runs over, the one named last changes fastest.
Arguments:
- offsets: float32 [4, 8, 32, 16, 3], P('gx', 'gy', 'gz'), may hold values from 0.2649 to 2.3351, as said below
- velocities: float32 [4, 8, 32, 16, 3], P('gx', 'gy', 'gz'), may hold values from -6 to 6
- occupied: int32 [4, 8, 32, 16], P('gx', 'gy', 'gz'), may hold values 0 or 1
Outputs:
- positions: float32 [4, 8, 32, 16, 3], P('gx', 'gy', 'gz')
- new_velocities: float32 [4, 8, 32, 16, 3], P('gx', 'gy', 'gz')
- forces: float32 [4, 8, 32, 16, 3], P('gx', 'gy', 'gz')
- capacity_history: float32 [4, 2], replicated
Inputs may be any that keep to these rules, and one draw needn't show every extreme that they name: `offsets`: each offset lies within the cell, a jittered body-centred lattice of 16 sites with spacing 1.3 per cell, jitter at most 0.06 in each coordinate.
All inputs are finite; a program needn't handle non-finite values.
Results may differ from a plain program's by a relative error of at most 0.0003.
Values sent between devices are 32-bit elements.
A program may use at most 128 MiB of HBM per device.

v0:
```python
import jax
import jax.numpy as jnp
from jax import lax
from jax.sharding import PartitionSpec as P

STEPS = 4


CUTOFF = 2.5
CELL_SIDE = 2.6
TIME_STEP = 0.005
BATH_STRENGTH = 0.25
GOAL_WARMTH = 0.8
FORCE_EDGE = 24.0 * (2.0 * CUTOFF ** (-13) - CUTOFF ** (-7))
ENERGY_EDGE = 4.0 * (CUTOFF ** (-12) - CUTOFF ** (-6))
STENCILS = [
    (along_x, along_y, along_z)
    for along_x in (-1, 0, 1)
    for along_y in (-1, 0, 1)
    for along_z in (-1, 0, 1)
]


def extended(cells, sides, width, closed):
    for axis, dim in sides:
        count = lax.axis_size(axis)
        ends = count if closed else count - 1
        head = lax.slice_in_dim(cells, 0, width, axis=dim)
        tail = lax.slice_in_dim(cells, cells.shape[dim] - width, cells.shape[dim], axis=dim)
        cells = jnp.concatenate(
            [
                lax.ppermute(tail, axis, [(i, (i + 1) % count) for i in range(ends)]),
                cells,
                lax.ppermute(head, axis, [((i + 1) % count, i) for i in range(ends)]),
            ],
            axis=dim,
        )
    return cells


def pair_terms(own_cells, neighbour, stencil):
    cell_shift = jnp.array(stencil, jnp.float32) * CELL_SIDE
    separation = neighbour[..., None, :, :3] + cell_shift - own_cells[..., :, None, :3]
    squared = jnp.sum(separation * separation, axis=-1)
    occupied_pair = own_cells[..., :, None, 3] * neighbour[..., None, :, 3]
    inside = (occupied_pair > 0.5) & (squared < CUTOFF * CUTOFF)
    if stencil == (0, 0, 0):
        slots_count = own_cells.shape[-2]
        inside = inside & jnp.logical_not(jnp.eye(slots_count, dtype=bool))
    guarded = jnp.where(inside, squared, 1.0)
    inverse = 1.0 / guarded
    inverse_six = inverse * inverse * inverse
    radius = jnp.sqrt(guarded)
    strength = (
        24.0 * (2.0 * inverse_six * inverse_six - inverse_six) * inverse - FORCE_EDGE / radius
    )
    strength = jnp.where(inside, strength, 0.0)
    energy = (
        4.0 * (inverse_six * inverse_six - inverse_six)
        - ENERGY_EDGE
        + (radius - CUTOFF) * FORCE_EDGE
    )
    energy = jnp.where(inside, energy, 0.0)
    pushes = -strength[..., None] * separation
    return (pushes, energy)


def window(padded, stencil, extent):
    return padded[
        1 + stencil[0] : 1 + stencil[0] + extent[0],
        1 + stencil[1] : 1 + stencil[1] + extent[1],
        1 + stencil[2] : 1 + stencil[2] + extent[2],
    ]


def full_forces(padded):
    extent = (padded.shape[0] - 2, padded.shape[1] - 2, padded.shape[2] - 2)
    own_cells = window(padded, (0, 0, 0), extent)
    forces = jnp.zeros(own_cells.shape[:-1] + (3,), jnp.float32)
    energy = jnp.zeros((), jnp.float32)
    for stencil in STENCILS:
        pushes, pair_energy = pair_terms(own_cells, window(padded, stencil, extent), stencil)
        forces = forces + jnp.sum(pushes, axis=-2)
        energy = energy + jnp.sum(pair_energy)
    return (forces, 0.5 * energy)


def evaluate(position, weight):
    packed = jnp.concatenate([position, weight[..., None]], axis=-1)
    padded = extended(packed, (("gx", 0), ("gy", 1), ("gz", 2)), 1, True)
    result = full_forces(padded)
    return result


def shards(offsets, velocities, occupied):
    weight = occupied.astype(jnp.float32)
    velocity = velocities * weight[..., None]
    position = offsets
    slot_total = float(
        offsets.shape[0]
        * offsets.shape[1]
        * offsets.shape[2]
        * offsets.shape[3]
        * lax.axis_size("gx")
        * lax.axis_size("gy")
        * lax.axis_size("gz")
    )
    forces, initial_energy = evaluate(position, weight)
    records = []
    for step_index in range(STEPS):
        velocity = velocity + 0.5 * TIME_STEP * forces
        position = position + TIME_STEP * velocity
        forces, potential = evaluate(position, weight)
        velocity = velocity + 0.5 * TIME_STEP * forces
        moving_vigor = 0.5 * jnp.sum(velocity * velocity)
        moving_vigor_sum, potential_all, body_tally = lax.psum(
            (moving_vigor, potential, jnp.sum(weight)), ("gx", "gy", "gz")
        )
        warmth_gauge = 2.0 * moving_vigor_sum / (3.0 * body_tally)
        speed_stretch = jnp.sqrt(1.0 + BATH_STRENGTH * (GOAL_WARMTH / warmth_gauge - 1.0))
        velocity = speed_stretch * velocity
        records.append(
            jnp.stack([potential_all, speed_stretch * speed_stretch * moving_vigor_sum])
            / slot_total
        )
    return (position, velocity, forces, jnp.stack(records))


def solution(mesh):
    in_specs = (
        P("gx", "gy", "gz", None, None),
        P("gx", "gy", "gz", None, None),
        P("gx", "gy", "gz", None),
    )
    out_specs = (
        P("gx", "gy", "gz", None, None),
        P("gx", "gy", "gz", None, None),
        P("gx", "gy", "gz", None, None),
        P(),
    )
    return jax.shard_map(shards, mesh=mesh, in_specs=in_specs, out_specs=out_specs, check_vma=False)
```

profile of v0, /device:TPU:0, one launch (start us, length us, event | category | flops | bytes accessed | tf_op | source)
XLA Modules:
  0.0 449.1 jit_solution(2037282775205533543)
XLA Ops:
  2.2 3.1 collective-permute-start.1
  5.4 1.8 collective-permute-done.1
  7.2 2.0 collective-permute-done
  11.5 2.3 collective-permute-done.2
  13.9 1.6 collective-permute-start.4
  15.5 2.2 collective-permute-start.5
  24.0 3.2 fusion.3
  31.1 2.2 fusion.9
  33.3 2.5 fusion.5
  35.8 2.5 fusion.7
  46.3 1.6 collective-permute-done.8
  49.5 2.6 collective-permute-start.11
  52.3 1.9 collective-permute-done.10
  57.2 3.6 fusion.57
  60.8 3.4 fusion.1129
  65.5 3.5 fusion.1124
  69.0 2.2 fusion.63
  71.2 2.5 fusion.59
  73.7 2.5 fusion.61
  77.7 40.2 %all-reduce.1 = (f32[]{:T(128)}, f32[]{:T(128)}) all-reduce(f32[]{:T(128)} %convert_reduce_fusion, f32[]{:T(128)S(6)} %mul.11654), channel_id=1, replica_groups=mesh['gx'=2,'gy'=4,'gz'=4] {'gx','gy','gz'}, use_global_device_ids=true, to_apply=%region_55.56 | all-reduce | flops 2 | bytes 16 | tf_op jit(solution)/shard_map/psum | solution.py:116
  119.4 2.6 collective-permute-start.13
  122.0 1.8 collective-permute-done.13
  123.9 2.0 collective-permute-done.12
  128.0 1.9 collective-permute-done.14
  130.3 2.0 collective-permute-start.16
  132.3 1.9 collective-permute-start.17
  134.4 1.7 collective-permute-done.16
  137.5 2.6 fusion.1119
  141.9 3.1 fusion.111
  147.0 3.4 fusion.1264
  150.5 3.4 fusion.1259
  153.9 2.2 fusion.117
  156.1 2.5 fusion.113
  158.6 2.5 fusion.115
  162.6 38.8 %psum.74 = f32[]{:T(128)} all-reduce(f32[]{:T(128)S(6)} %mul.12010), channel_id=1, replica_groups=mesh['gx'=2,'gy'=4,'gz'=4] {'gx','gy','gz'}, use_global_device_ids=true, to_apply=%region_167.168 | all-reduce | flops 1 | bytes 8 | tf_op jit(solution)/shard_map/psum | solution.py:116
  202.3 2.6 collective-permute-start.19
  204.9 1.8 collective-permute-done.19
  206.7 2.0 collective-permute-done.18
  211.4 1.7 collective-permute-done.20
  214.1 2.1 collective-permute-start.22
  216.3 1.7 collective-permute-start.23
  218.2 1.7 collective-permute-done.22
  224.6 2.6 fusion.1254
  227.3 3.0 fusion.165
  232.1 3.5 fusion.1399
  235.6 2.2 fusion.171
  237.8 3.5 fusion.1394
  241.3 2.5 fusion.167
  243.8 2.5 fusion.169
  247.9 39.0 %psum.75 = f32[]{:T(128)} all-reduce(f32[]{:T(128)S(6)} %mul.12366), channel_id=1, replica_groups=mesh['gx'=2,'gy'=4,'gz'=4] {'gx','gy','gz'}, use_global_device_ids=true, to_apply=%region_223.224 | all-reduce | flops 1 | bytes 8 | tf_op jit(solution)/shard_map/psum | solution.py:116
  287.7 2.6 collective-permute-start.25
  319.5 2.3 collective-permute-done.26
  323.0 2.0 collective-permute-start.28
  325.0 1.9 collective-permute-start.29
  327.1 1.7 collective-permute-done.28
  333.5 3.1 fusion.219
  336.6 2.6 fusion.1389
  339.2 3.6 fusion.1064
  342.9 3.4 fusion.1479
  346.3 2.2 fusion.225
  348.5 3.2 fusion.1474
  351.7 2.5 fusion.221
  354.2 2.7 fusion.223
  401.5 41.6 %all-reduce = (f32[]{:T(128)}, f32[1,1]{0,1:T(1,128)}, f32[1,1]{0,1:T(1,128)}, f32[1,1]{0,1:T(1,128)}, f32[1,1]{0,1:T(1,128)}) all-reduce(f32[]{:T(128)S(6)} %mul.12722, f32[1,1]{0,1:T(1,128)} %bitcast.137, f32[1,1]{0,1:T(1,128)} %bitcast.135, f32[1,1]{0,1:T(1,128)} %bitcast.133, ...), channel_id=1, replica_groups=mesh['gx'=2,'gy'=4,'gz'=4] {'gx','gy','gz'}, use_global_device_ids=true, to_apply=%region_279.280 | all-reduce | flops 5 | bytes 40 | tf_op jit(solution)/shard_map/psum | solution.py:116
  (359 shorter events, 62.6 us)
Async XLA Ops:
  2.2 5.0 %collective-permute-start.1 = (f32[1,2,8,16,4]{3,4,2,1,0:T(4,128)S(1)}, f32[1,2,8,16,4]{3,4,2,1,0:T(4,128)S(1)}, u32[]{:S(2)}, u32[]{:S(2)}) collective-permute-start(f32[1,2,8,16,4]{3,4,2,1,0:T(4,128)S(1)} %get-tuple-element.779), channel_id=1, source_target_pairs={{16,0},{0,16},{17,1},{1,17},{18,2},{2,18},{19,3},{3,19},{20,4},{4,... | collective-permute-start | bytes 12296 | tf_op jit(solution)/shard_map/ppermute | solution.py:34
  5.3 3.9 collective-permute-start
  5.4 58.7 %copy-start.21 = (pred[16,16]{1,0:T(8,128)(4,1)}, pred[16,16]{1,0:T(8,128)(4,1)S(1)}, u32[]{:S(2)}) copy-start(pred[16,16]{1,0:T(8,128)(4,1)S(1)} %fusion.1753) | copy-start | bytes 772
  9.3 2.2 collective-permute-start.3
  9.4 4.4 collective-permute-start.2
  13.9 5.8 %collective-permute-start.4 = (f32[4,4,1,16,4]{3,4,2,1,0:T(4,128)S(1)}, f32[4,4,1,16,4]{3,4,2,1,0:T(4,128)S(1)}, u32[]{:S(2)}, u32[]{:S(2)}) collective-permute-start(f32[4,4,1,16,4]{3,4,2,1,0:T(4,128)S(1)} %get-tuple-element.678), channel_id=1, source_target_pairs={{0,1},{1,2},{2,3},{3,0},{4,5},{5,6},{6,7},{7,4},{8,9},{9,10},{10,1... | collective-permute-start | bytes 12296 | tf_op jit(solution)/shard_map/ppermute | solution.py:32
  15.5 4.3 collective-permute-start.5
  35.8 2.5 copy-start.25
  39.4 2.2 copy-start.24
  39.5 4.0 collective-permute-start.7
  40.1 3.9 collective-permute-start.6
  44.1 2.2 collective-permute-start.9
  44.1 3.7 collective-permute-start.8
  48.3 5.9 %collective-permute-start.10 = (f32[4,4,1,16,4]{3,4,2,1,0:T(4,128)S(1)}, f32[4,4,1,16,4]{3,4,2,1,0:T(4,128)S(1)}, u32[]{:S(2)}, u32[]{:S(2)}) collective-permute-start(f32[4,4,1,16,4]{3,4,2,1,0:T(4,128)S(1)} %get-tuple-element.676), channel_id=1, source_target_pairs={{0,1},{1,2},{2,3},{3,0},{4,5},{5,6},{6,7},{7,4},{8,9},{9,10},{10,1... | collective-permute-start | bytes 12296 | tf_op jit(solution)/shard_map/ppermute | solution.py:32
  49.5 4.6 %collective-permute-start.11 = (f32[4,4,1,16,4]{3,4,2,1,0:T(4,128)S(1)}, f32[4,4,1,16,4]{3,4,2,1,0:T(4,128)S(1)}, u32[]{:S(2)}, u32[]{:S(2)}) collective-permute-start(f32[4,4,1,16,4]{3,4,2,1,0:T(4,128)S(1)} %get-tuple-element.677), channel_id=1, source_target_pairs={{1,0},{2,1},{3,2},{0,3},{5,4},{6,5},{7,6},{4,7},{9,8},{10,9},{11,1... | collective-permute-start | bytes 12296 | tf_op jit(solution)/shard_map/ppermute | solution.py:34
  119.4 4.5 collective-permute-start.13
  122.0 3.9 collective-permute-start.12
  126.0 2.0 collective-permute-start.15
  126.0 3.9 collective-permute-start.14
  127.0 18.1 %copy-start.17 = (f32[2,2,8,16,1]{3,4,2,1,0:T(1,128)}, f32[2,2,8,16,1]{3,4,2,1,0:T(1,128)S(1)}, u32[]{:S(2)}) copy-start(f32[2,2,8,16,1]{3,4,2,1,0:T(1,128)S(1)} %slice.1844) | copy-start | bytes 6148
  130.2 14.9 %copy-start.19 = (f32[2,2,8,16,1]{3,4,2,1,0:T(1,128)}, f32[2,2,8,16,1]{3,4,2,1,0:T(1,128)S(1)}, u32[]{:S(2)}) copy-start(f32[2,2,8,16,1]{3,4,2,1,0:T(1,128)S(1)} %get-tuple-element.708) | copy-start | bytes 6148
  130.3 5.8 %collective-permute-start.16 = (f32[4,4,1,16,4]{3,4,2,1,0:T(4,128)S(1)}, f32[4,4,1,16,4]{3,4,2,1,0:T(4,128)S(1)}, u32[]{:S(2)}, u32[]{:S(2)}) collective-permute-start(f32[4,4,1,16,4]{3,4,2,1,0:T(4,128)S(1)} %get-tuple-element.674), channel_id=1, source_target_pairs={{0,1},{1,2},{2,3},{3,0},{4,5},{5,6},{6,7},{7,4},{8,9},{9,10},{10,1... | collective-permute-start | bytes 12296 | tf_op jit(solution)/shard_map/ppermute | solution.py:32
  132.3 4.1 collective-permute-start.17
  136.9 8.2 %copy-start.7 = (f32[2,2,8,16,1]{3,4,2,1,0:T(1,128)}, f32[2,2,8,16,1]{3,4,2,1,0:T(1,128)S(1)}, u32[]{:S(2)}) copy-start(f32[2,2,8,16,1]{3,4,2,1,0:T(1,128)S(1)} %get-tuple-element.561) | copy-start | bytes 6148
  136.9 8.2 %copy-start.9 = (f32[2,2,8,16,1]{3,4,2,1,0:T(1,128)}, f32[2,2,8,16,1]{3,4,2,1,0:T(1,128)S(1)}, u32[]{:S(2)}) copy-start(f32[2,2,8,16,1]{3,4,2,1,0:T(1,128)S(1)} %get-tuple-element.562) | copy-start | bytes 6148
  136.9 8.2 %copy-start.11 = (f32[2,2,8,16,1]{3,4,2,1,0:T(1,128)}, f32[2,2,8,16,1]{3,4,2,1,0:T(1,128)S(1)}, u32[]{:S(2)}) copy-start(f32[2,2,8,16,1]{3,4,2,1,0:T(1,128)S(1)} %get-tuple-element.563) | copy-start | bytes 6148
  137.2 7.9 %copy-start.13 = (f32[2,2,8,16,1]{3,4,2,1,0:T(1,128)}, f32[2,2,8,16,1]{3,4,2,1,0:T(1,128)S(1)}, u32[]{:S(2)}) copy-start(f32[2,2,8,16,1]{3,4,2,1,0:T(1,128)S(1)} %get-tuple-element.553) | copy-start | bytes 6148
  137.2 7.9 %copy-start.15 = (f32[2,2,8,16,1]{3,4,2,1,0:T(1,128)}, f32[2,2,8,16,1]{3,4,2,1,0:T(1,128)S(1)}, u32[]{:S(2)}) copy-start(f32[2,2,8,16,1]{3,4,2,1,0:T(1,128)S(1)} %get-tuple-element.554) | copy-start | bytes 6148
  141.7 3.5 copy-start
  141.7 3.5 copy-start.2
  145.1 2.0 copy-start.4
  202.3 4.4 collective-permute-start.19
  204.8 3.9 collective-permute-start.18
  208.8 2.5 collective-permute-start.21
  208.9 4.1 collective-permute-start.20
  214.1 5.8 %collective-permute-start.22 = (f32[4,4,1,16,4]{3,4,2,1,0:T(4,128)S(1)}, f32[4,4,1,16,4]{3,4,2,1,0:T(4,128)S(1)}, u32[]{:S(2)}, u32[]{:S(2)}) collective-permute-start(f32[4,4,1,16,4]{3,4,2,1,0:T(4,128)S(1)} %get-tuple-element.672), channel_id=1, source_target_pairs={{0,1},{1,2},{2,3},{3,0},{4,5},{5,6},{6,7},{7,4},{8,9},{9,10},{10,1... | collective-permute-start | bytes 12296 | tf_op jit(solution)/shard_map/ppermute | solution.py:32
  216.3 1.7 copy-start.68
  216.3 1.7 copy-start.71
  216.3 1.7 copy-start.74
  216.3 4.0 collective-permute-start.23
  218.0 2.4 copy-start.53
  218.0 2.4 copy-start.56
  218.0 2.4 copy-start.59
  218.0 2.4 copy-start.62
  218.1 2.4 copy-start.65
  222.9 1.7 copy-start.1
  222.9 1.7 copy-start.3
  222.9 1.7 copy-start.8
  222.9 1.6 copy-start.10
  287.7 29.4 %collective-permute-start.25 = (f32[1,2,8,16,4]{3,4,2,1,0:T(4,128)S(1)}, f32[1,2,8,16,4]{3,4,2,1,0:T(4,128)S(1)}, u32[]{:S(2)}, u32[]{:S(2)}) collective-permute-start(f32[1,2,8,16,4]{3,4,2,1,0:T(4,128)S(1)} %get-tuple-element.763), channel_id=1, source_target_pairs={{16,0},{0,16},{17,1},{1,17},{18,2},{2,18},{19,3},{3,19},{20,4},{4,... | collective-permute-start | bytes 12296 | tf_op jit(solution)/shard_map/ppermute | solution.py:34
  290.3 26.9 %collective-permute-start.24 = (f32[1,2,8,16,4]{3,4,2,1,0:T(4,128)S(1)}, f32[1,2,8,16,4]{3,4,2,1,0:T(4,128)S(1)}, u32[]{:S(2)}, u32[]{:S(2)}) collective-permute-start(f32[1,2,8,16,4]{3,4,2,1,0:T(4,128)S(1)} %get-tuple-element.762), channel_id=1, source_target_pairs={{0,16},{16,0},{1,17},{17,1},{2,18},{18,2},{3,19},{19,3},{4,20},{20... | collective-permute-start | bytes 12296 | tf_op jit(solution)/shard_map/ppermute | solution.py:32
  317.2 2.3 collective-permute-start.27
  317.3 4.6 %collective-permute-start.26 = (f32[4,1,8,16,4]{3,4,2,1,0:T(4,128)S(1)}, f32[4,1,8,16,4]{3,4,2,1,0:T(4,128)S(1)}, u32[]{:S(2)}, u32[]{:S(2)}) collective-permute-start(f32[4,1,8,16,4]{3,4,2,1,0:T(4,128)S(1)} %get-tuple-element.751), channel_id=1, source_target_pairs={{0,4},{4,8},{8,12},{12,0},{1,5},{5,9},{9,13},{13,1},{2,6},{6,10},{... | collective-permute-start | bytes 24584 | tf_op jit(solution)/shard_map/ppermute | solution.py:32
  322.8 6.5 %copy-start.54 = (f32[3]{0:T(128)S(1)}, f32[3]{0:T(128)}, u32[]{:S(2)}) copy-start(f32[3]{0:T(128)} %constant.364) | copy-start | bytes 40
  322.8 6.5 %copy-start.57 = (f32[3]{0:T(128)S(1)}, f32[3]{0:T(128)}, u32[]{:S(2)}) copy-start(f32[3]{0:T(128)} %constant.361) | copy-start | bytes 40
  322.9 6.5 %copy-start.60 = (f32[3]{0:T(128)S(1)}, f32[3]{0:T(128)}, u32[]{:S(2)}) copy-start(f32[3]{0:T(128)} %constant.358) | copy-start | bytes 40
  322.9 6.5 %copy-start.63 = (f32[3]{0:T(128)S(1)}, f32[3]{0:T(128)}, u32[]{:S(2)}) copy-start(f32[3]{0:T(128)} %constant.355) | copy-start | bytes 40
  322.9 6.5 %copy-start.66 = (f32[3]{0:T(128)S(1)}, f32[3]{0:T(128)}, u32[]{:S(2)}) copy-start(f32[3]{0:T(128)} %constant.352) | copy-start | bytes 40
  323.0 5.8 %collective-permute-start.28 = (f32[4,4,1,16,4]{3,4,2,1,0:T(4,128)S(1)}, f32[4,4,1,16,4]{3,4,2,1,0:T(4,128)S(1)}, u32[]{:S(2)}, u32[]{:S(2)}) collective-permute-start(f32[4,4,1,16,4]{3,4,2,1,0:T(4,128)S(1)} %get-tuple-element.670), channel_id=1, source_target_pairs={{0,1},{1,2},{2,3},{3,0},{4,5},{5,6},{6,7},{7,4},{8,9},{9,10},{10,1... | collective-permute-start | bytes 12296 | tf_op jit(solution)/shard_map/ppermute | solution.py:32
  325.0 1.9 copy-start.69
  325.0 1.9 copy-start.72
  325.0 1.9 copy-start.75
  325.0 4.1 collective-permute-start.29
  336.6 2.6 copy-start.5
  (57 other events, 43.0 us)
where the time goes:
time: 455 us; the launch traced here: 449 us
  blocking collectives  160 us (35%)
  other arithmetic  124 us (27%)
  between operations  78.7 us (17%)
  starting transfers between devices  36 us (8%)
  waiting for transfers between devices  33.8 us (7%)
  local copies, waits for them, and re-layouts  16.8 us (4%)
    psum x4, blocking collectives, shards(): lax.psum((moving_vigor, potential, jnp.sum(weight)), ('gx', 'gy', 'gz'))  160 us
    reduce_sum x20, other arithmetic, full_forces(): forces = forces + jnp.sum(pushes, axis=-2)  52.1 us
    reduce_sum x12, other arithmetic, full_forces(): energy = energy + jnp.sum(pair_energy)  38.9 us
    ppermute x15, waiting for transfers between devices, extended(): lax.ppermute(tail, axis, [(i, (i + 1) % count) for i in range(ends)])  23.5 us
    ppermute x15, starting transfers between devices, extended(): lax.ppermute(head, axis, [((i + 1) % count, i) for i in range(ends)])  22 us
    unnamed x186, local copies, waits for them, and re-layouts  15 us
    ppermute x15, starting transfers between devices, extended(): lax.ppermute(tail, axis, [(i, (i + 1) % count) for i in range(ends)])  14 us
    ppermute x15, waiting for transfers between devices, extended(): lax.ppermute(head, axis, [((i + 1) % count, i) for i in range(ends)])  10.3 us
  transfers between devices with their start and end apart: 30, of which 24 were waited for; matrix products, arithmetic and copies ran while one was open for 1% of the time, Pallas kernels for 0%

commit v1 on v0

v1 whole, which is shorter than its diff:
```python
import functools

import jax
import jax.numpy as jnp
from jax import lax
from jax.experimental import pallas as pl
from jax.experimental.pallas import tpu as pltpu
from jax.sharding import PartitionSpec as P

MESH = pl.DeviceIdType.MESH
STEPS = 4
CUTOFF = 2.5
CELL_SIDE = 2.6
TIME_STEP = 0.005
BATH_STRENGTH = 0.25
GOAL_WARMTH = 0.8
FORCE_EDGE = 24.0 * (2.0 * CUTOFF ** (-13) - CUTOFF ** (-7))
ENERGY_EDGE = 4.0 * (CUTOFF ** (-12) - CUTOFF ** (-6))
FAR = 1.0e15


def offsets_of(size):
    return [0] if size == 1 else [0, 1] if size == 2 else [0, 1, -1]


def kernel(
    axes, shape, o_in, v_in, occ_in, o_out, v_out, f_out, h_out,
    ostate, vstate, near, osend, orecv, fsend, frecv, kbuf, tally, stretch,
    o_send_sem, o_recv_sem, f_send_sem, f_recv_sem, k_send_sem, k_recv_sem,
):
    gx, gy, gz = axes
    nx, ny, nz, slots = shape
    lanes = nz * slots
    tile = fsend.shape[2]
    devices = gx * gy * gz
    slot_total = float(devices * nx * ny * lanes)
    me = [lax.axis_index(a) for a in ("gx", "gy", "gz")]
    my_id = (me[0] * gy + me[1]) * gz + me[2]

    def device(j):
        d = lax.rem(my_id + j, devices)
        return (d // (gy * gz), lax.rem(d // gz, gy), lax.rem(d, gz))

    def canonical(size, off):
        return 0 if size == 1 else off % 2 if size == 2 else off

    def padded(size, n):
        return (
            [(canonical(size, -1), n - 1)]
            + [(0, i) for i in range(n)]
            + [(canonical(size, 1), 0)]
        )

    px_of, py_of = padded(gx, nx), padded(gy, ny)
    xs = offsets_of(gx)
    partners = [
        (a, b, c) for a in xs for b in offsets_of(gy) for c in offsets_of(gz) if (a, b, c) != (0, 0, 0)
    ]
    slot_of = {d: i for i, d in enumerate(partners)}

    def layers_of(b):
        return sorted({yl for off, yl in py_of if off == b})

    def halo_copies(src, dst, send_sem, recv_sem):
        copies = []
        for i, (a, b, c) in enumerate(partners):
            to = (
                lax.rem(me[0] - a + gx, gx), lax.rem(me[1] - b + gy, gy), lax.rem(me[2] - c + gz, gz),
            )
            need = layers_of(b)
            where = pl.ds(need[0], need[-1] - need[0] + 1)
            copies.append(
                pltpu.make_async_remote_copy(
                    src_ref=src.at[where], dst_ref=dst.at[i, where],
                    send_sem=send_sem.at[i], recv_sem=recv_sem.at[i],
                    device_id=to, device_id_type=MESH,
                )
            )
        return copies

    barrier = pltpu.get_barrier_semaphore()

    def greet(j, _):
        pl.semaphore_signal(barrier, inc=1, device_id=device(j), device_id_type=MESH)
        return 0

    lax.fori_loop(1, devices, greet, 0)

    lane = lax.broadcasted_iota(jnp.int32, (nz, lanes), 1)
    level = lax.broadcasted_iota(jnp.int32, (nz, lanes), 0)
    spread = (
        lax.rem(lax.broadcasted_iota(jnp.int32, (slots, lanes), 1), slots)
        == lax.broadcasted_iota(jnp.int32, (slots, lanes), 0)
    ).astype(jnp.float32)

    def rows_of(planes):
        flat = planes.reshape(-1, slots)
        wide = jnp.dot(flat, spread, precision=lax.Precision.HIGHEST, preferred_element_type=jnp.float32)
        wide = wide.reshape(-1, nz, lanes)
        return jnp.sum(jnp.where((lane // slots == level)[None], wide, 0.0), axis=1)

    o_rows = rows_of(o_in[...])
    v_rows = rows_of(v_in[...])
    w_rows = rows_of(occ_in[...].astype(jnp.float32))
    osend[...] = jnp.zeros_like(osend)
    fsend[...] = jnp.zeros_like(fsend)
    for x in range(nx):
        for y in range(ny):
            w = w_rows[x * ny + y : x * ny + y + 1]
            for c in range(3):
                i = (x * ny + y) * 3 + c
                r = c * nx + x
                osend[y, 0, r : r + 1] = jnp.where(w > 0.5, o_rows[i : i + 1], FAR)
                osend[y, 1, r : r + 1] = v_rows[i : i + 1] * w
    tally[...] = jnp.sum(w_rows, axis=0, keepdims=True)

    pl.semaphore_wait(barrier, devices - 1)
    first = halo_copies(osend, orecv, o_send_sem, o_recv_sem)
    for copy in first:
        copy.start()
    for copy in first:
        copy.wait()

    edge_lane = lax.broadcasted_iota(jnp.int32, (tile, lanes), 1)

    def columns(own, received):
        found = {}
        for xi, a in enumerate(xs):
            for py, (b, yl) in enumerate(py_of):
                def block(c):
                    d = (a, b, canonical(gz, c))
                    return own(yl) if d == (0, 0, 0) else received(slot_of[d], yl)

                mid = block(0)
                found[xi, py, 1] = mid
                low = jnp.where(edge_lane >= lanes - slots, block(-1), mid)
                found[xi, py, 0] = pltpu.roll(low, slots, 1)
                high = jnp.where(edge_lane < slots, block(1), mid)
                found[xi, py, 2] = pltpu.roll(high, lanes - slots, 1)
        return found

    for q, state in enumerate((ostate, vstate)):
        found = columns(lambda yl: osend[yl, q], lambda s, yl: orecv[s, yl, q])
        for (xi, py, dz), value in found.items():
            state[xi, py, dz] = value

    row_id = lax.broadcasted_iota(jnp.int32, (2 * 8, lanes), 0)
    lane_id = lax.broadcasted_iota(jnp.int32, (slots, lanes), 1)
    slot_id = lax.broadcasted_iota(jnp.int32, (slots, lanes), 0)
    pick = (lane_id // slots) * slots + slot_id
    itself = lax.rem(lane_id, slots) == slot_id

    def nearby(py, _):
        for px, (a, xl) in enumerate(px_of):
            for dz in range(3):
                block = ostate[xs.index(a), py, dz]
                for c in range(3):
                    r = c * nx + xl
                    row = jnp.broadcast_to(block[r : r + 1], (slots, lanes))
                    near[px, py, dz, c] = jnp.take_along_axis(row, pick, axis=1, mode="promise_in_bounds")
        return 0

    def out_planes(block, ref, y, mask):
        at = lax.broadcasted_iota(jnp.int32, (nz, lanes), 0) * slots + lax.rem(lane, slots)
        for x in range(nx):
            for c in range(3):
                r = c * nx + x
                row = jnp.broadcast_to(block[r : r + 1], (nz, lanes))
                plane = jnp.take_along_axis(row, at, axis=1, mode="promise_in_bounds")[:, :slots]
                if mask:
                    plane = jnp.where(occ_in[x, y] > 0, plane, o_in[x, y, c])
                ref[x, y, c] = plane

    half = 0.5 * TIME_STEP

    def step(k, _):
        p = lax.rem(k, 2)
        lax.fori_loop(0, ny + 2, nearby, 0)

        energy_rows = jnp.zeros((1, lanes), jnp.float32)
        for x in range(nx):
            def one_row(y, carried):
                block = ostate[0, y + 1, 1]
                mine = [block[c * nx + x : c * nx + x + 1] for c in range(3)]
                occupied = mine[0] < 0.5 * FAR
                force = [jnp.zeros((slots, lanes), jnp.float32) for _ in range(3)]
                energy = jnp.zeros((slots, lanes), jnp.float32)
                for dx in (-1, 0, 1):
                    for dy in (-1, 0, 1):
                        for dz in (-1, 0, 1):
                            shift = (dx, dy, dz)
                            apart = [
                                near[x + 1 + dx, y + 1 + dy, dz + 1, c] - (mine[c] - shift[c] * CELL_SIDE)
                                for c in range(3)
                            ]
                            squared = apart[0] * apart[0] + apart[1] * apart[1] + apart[2] * apart[2]
                            if shift == (0, 0, 0):
                                squared = jnp.where(itself, FAR, squared)
                            inside = squared < CUTOFF * CUTOFF
                            inv = lax.rsqrt(squared)
                            inv2 = inv * inv
                            inv6 = inv2 * inv2 * inv2
                            pull = inv * (FORCE_EDGE - inv * inv6 * (48.0 * inv6 - 24.0))
                            pull = jnp.where(inside, pull, 0.0)
                            for c in range(3):
                                force[c] = force[c] + pull * apart[c]
                            bond = inv6 * (4.0 * inv6 - 4.0) + (
                                squared * inv * FORCE_EDGE - (ENERGY_EDGE + CUTOFF * FORCE_EDGE)
                            )
                            energy = energy + jnp.where(inside, bond, 0.0)
                for c in range(3):
                    total = jnp.sum(force[c], axis=0, keepdims=True)
                    fsend[p, y, c * nx + x : c * nx + x + 1] = jnp.where(occupied, total, 0.0)
                total = jnp.sum(energy, axis=0, keepdims=True)
                return carried + jnp.where(occupied, total, 0.0)

            energy_rows = lax.fori_loop(0, ny, one_row, energy_rows)

        kinetic = jnp.zeros((tile, lanes), jnp.float32)
        for y in range(ny):
            v = vstate[0, y + 1, 1] + half * fsend[p, y]
            kinetic = kinetic + v * v
        kinetic = 0.5 * jnp.sum(kinetic, axis=0, keepdims=True)
        kbuf[p, my_id, 0:1] = jnp.where(k == 0, tally[...], kinetic)
        kbuf[p, my_id, 1:2] = 0.5 * energy_rows

        def k_copy(j):
            return pltpu.make_async_remote_copy(
                src_ref=kbuf.at[p, my_id], dst_ref=kbuf.at[p, my_id],
                send_sem=k_send_sem.at[j - 1], recv_sem=k_recv_sem.at[p, j - 1],
                device_id=device(j), device_id_type=MESH,
            )

        def start(j, _):
            k_copy(j).start()
            return 0

        def finish(j, _):
            k_copy(j).wait()
            return 0

        halo = halo_copies(fsend.at[p], frecv.at[p], f_send_sem, f_recv_sem.at[p])

        @pl.when(k < STEPS)
        def _():
            for copy in halo:
                copy.start()

        lax.fori_loop(1, devices, start, 0)

        @pl.when(k == STEPS)
        def _():
            for y in range(ny):
                out_planes(ostate[0, y + 1, 1], o_out, y, True)
                out_planes(fsend[p, y], f_out, y, False)

        lax.fori_loop(1, devices, finish, 0)

        @pl.when(k < STEPS)
        def _():
            for copy in halo:
                copy.wait()

        everyone = jnp.sum(kbuf[p], axis=0)
        totals = jnp.sum(everyone, axis=1, keepdims=True)
        vigor, potential = totals[0:1], totals[1:2]

        @pl.when(k == 0)
        def _():
            tally[...] = jnp.broadcast_to(vigor, (1, lanes))
            stretch[...] = jnp.ones_like(stretch)

        @pl.when(k > 0)
        def _():
            warmth = 2.0 * jnp.broadcast_to(vigor, (1, lanes)) / (3.0 * tally[...])
            lam = jnp.sqrt(1.0 + BATH_STRENGTH * (GOAL_WARMTH / warmth - 1.0))
            stretch[...] = lam
            which = lax.broadcasted_iota(jnp.int32, (1, lanes), 1)
            record = jnp.where(which == 0, potential, lam * lam * vigor) / slot_total
            h_out[pl.ds(k - 1, 1), :] = record[:, :2]

        lam = stretch[...]
        before = jnp.where(k > 0, half, 0.0)

        @pl.when(k < STEPS)
        def _():
            found = columns(lambda yl: fsend[p, yl], lambda s, yl: frecv[p, s, yl])
            for (xi, py, dz), f in found.items():
                v = (vstate[xi, py, dz] + before * f) * lam
                v = v + half * f
                vstate[xi, py, dz] = v
                ostate[xi, py, dz] = ostate[xi, py, dz] + TIME_STEP * v

        @pl.when(k == STEPS)
        def _():
            for y in range(ny):
                v = (vstate[0, y + 1, 1] + half * fsend[p, y]) * lam
                out_planes(v, v_out, y, False)

        return 0

    lax.fori_loop(0, STEPS + 1, step, 0)


def shards(axes, offsets, velocities, occupied):
    gx, gy, gz = axes
    nx, ny, nz, slots = occupied.shape
    lanes = nz * slots
    tile = -(-3 * nx // 8) * 8
    nxo, nyo, nzo = (len(offsets_of(s)) for s in axes)
    halo = nxo * nyo * nzo - 1
    devices = gx * gy * gz
    f32 = jnp.float32
    plane = jax.ShapeDtypeStruct((nx, ny, 3, nz, slots), f32)
    vmem = pl.BlockSpec(memory_space=pltpu.VMEM)
    dma = pltpu.SemaphoreType.DMA
    o, v, f, h = pl.pallas_call(
        functools.partial(kernel, axes, (nx, ny, nz, slots)),
        name="verlet",
        out_shape=[plane, plane, plane, jax.ShapeDtypeStruct((STEPS, 2), f32)],
        in_specs=[vmem] * 3,
        out_specs=[vmem] * 4,
        scratch_shapes=[
            pltpu.VMEM((nxo, ny + 2, 3, tile, lanes), f32),
            pltpu.VMEM((nxo, ny + 2, 3, tile, lanes), f32),
            pltpu.VMEM((nx + 2, ny + 2, 3, 3, slots, lanes), f32),
            pltpu.VMEM((ny, 2, tile, lanes), f32),
            pltpu.VMEM((halo, ny, 2, tile, lanes), f32),
            pltpu.VMEM((2, ny, tile, lanes), f32),
            pltpu.VMEM((2, halo, ny, tile, lanes), f32),
            pltpu.VMEM((2, devices, 2, lanes), f32),
            pltpu.VMEM((1, lanes), f32),
            pltpu.VMEM((1, lanes), f32),
            dma((halo,)),
            dma((halo,)),
            dma((halo,)),
            dma((2, halo)),
            dma((devices - 1,)),
            dma((2, devices - 1)),
        ],
        compiler_params=pltpu.CompilerParams(collective_id=0, has_side_effects=True),
    )(
        jnp.transpose(offsets, (0, 1, 4, 2, 3)),
        jnp.transpose(velocities, (0, 1, 4, 2, 3)),
        occupied,
    )
    back = (0, 1, 3, 4, 2)
    return (jnp.transpose(o, back), jnp.transpose(v, back), jnp.transpose(f, back), h)


def solution(mesh):
    axes = tuple(mesh.shape[a] for a in ("gx", "gy", "gz"))
    in_specs = (
        P("gx", "gy", "gz", None, None),
        P("gx", "gy", "gz", None, None),
        P("gx", "gy", "gz", None),
    )
    out_specs = (
        P("gx", "gy", "gz", None, None),
        P("gx", "gy", "gz", None, None),
        P("gx", "gy", "gz", None, None),
        P(),
    )
    return jax.shard_map(
        functools.partial(shards, axes), mesh=mesh, in_specs=in_specs, out_specs=out_specs, check_vma=False
    )
```

time: 455 us -> 59.3 us (0.13); the launches traced: 449 us -> 58.9 us
  blocking collectives: 160 us -> 0 us
  other arithmetic: 124 us -> 0 us
  between operations: 78.7 us -> 0.65 us
  Pallas kernels: 0 us -> 54.1 us
  starting transfers between devices: 36 us -> 0 us
  waiting for transfers between devices: 33.8 us -> 0 us
  local copies, waits for them, and re-layouts: 16.8 us -> 4.16 us
    psum x4 -> x0, blocking collectives: 160 us -> none  [shards(): lax.psum((moving_vigor, potential, jnp.sum(weight)), ('gx', 'gy', 'gz'))]
    reduce_sum x47 -> x0, other arithmetic: 104 us -> none  [the longest x20 52.1 us: full_forces(): forces = forces + jnp.sum(pushes, axis=-2)]
    pallas_call x0 -> x1, Pallas kernels: none -> 54.1 us  [shards(): pl.pallas_call(functools.partial(kernel, axes, (nx, ny, nz, slots)), name...]
    ppermute x30 -> x0, starting transfers between devices: 36 us -> none  [the longest x15 22 us: extended(): lax.ppermute(head, axis, [((i + 1) % count, i) for i in range(ends)])]
    ppermute x30 -> x0, waiting for transfers between devices: 33.8 us -> none  [the longest x15 23.5 us: extended(): lax.ppermute(tail, axis, [(i, (i + 1) % count) for i in range(ends)])]
    unnamed x186 -> x10, local copies, waits for them, and re-layouts: 15 us -> 4.16 us
    neg x14 -> x0, other arithmetic: 9.49 us -> none  [pair_terms(): pushes = -strength[..., None] * separation]
  transfers between devices with their start and end apart: 30 -> 0, of which waited for: 24 -> 0; matrix products, arithmetic and copies ran while one was open for 1% -> 0% of each run, Pallas kernels for 0% -> 0%
where the time goes in v1:
time: 59.3 us; the launch traced here: 58.9 us
  Pallas kernels  54.1 us (91%)
  local copies, waits for them, and re-layouts  4.16 us (7%)
  between operations  0.65 us (1%)
    pallas_call x1, Pallas kernels, shards(): pl.pallas_call(functools.partial(kernel, axes, (nx, ny, nz, slots)), name...  54.1 us
    unnamed x10, local copies, waits for them, and re-layouts  4.16 us

profile of v1, /device:TPU:0, one launch (start us, length us, event | category | flops | bytes accessed | tf_op | source)
XLA Modules:
  0.0 58.9 jit_solution(17021054164660526031)
XLA Ops:
  0.6 54.1 %verlet.1 = (f32[2,2,3,8,16]{4,3,2,1,0:T(8,128)}, f32[2,2,3,8,16]{4,3,2,1,0:T(8,128)}, f32[2,2,3,8,16]{4,3,2,1,0:T(8,128)}, f32[4,2]{1,0:T(4,128)}) custom-call(f32[2,2,3,8,16]{4,3,2,1,0:T(8,128)} %bitcast.5, f32[2,2,3,8,16]{4,3,2,1,0:T(8,128)} %bitcast.6, s32[2,2,8,16]{3,2,1,0:T(8,128)} %occ_in.1), custom_call_target="tpu_custom_call" | custom-call | tf_op jit(solution)/shard_map/verlet/pallas_call | solution.py:317
  54.8 0.0 copy-start.2
  54.8 0.6 %copy-done.2 = f32[4,2]{1,0:T(4,128)S(1)} copy-done((f32[4,2]{1,0:T(4,128)S(1)}, f32[4,2]{1,0:T(4,128)}, u32[]{:S(2)}) %copy-start.2) | copy-done | bytes 56
  55.4 0.6 %copy.7 = f32[4,2]{0,1:T(2,128)} copy(f32[4,2]{1,0:T(4,128)S(1)} %copy-done.2) | data formatting | bytes 64
  56.1 0.0 copy-start.1
  56.1 1.4 %copy.11 = f32[2,2,8,16,3]{3,2,4,1,0:T(8,128)} copy(f32[2,2,8,16,3]{3,2,4,1,0:T(8,128)} %bitcast.9) | data formatting | bytes 12288
  57.5 0.0 copy-done.1
  57.5 0.0 copy-start
  57.5 0.6 %copy.12 = f32[2,2,8,16,3]{3,2,4,1,0:T(8,128)} copy(f32[2,2,8,16,3]{3,2,4,1,0:T(8,128)S(1)} %bitcast.8) | data formatting | bytes 12288
  58.1 0.2 copy-done
  58.3 0.6 %copy.13 = f32[2,2,8,16,3]{3,2,4,1,0:T(8,128)} copy(f32[2,2,8,16,3]{3,2,4,1,0:T(8,128)S(1)} %bitcast.7) | data formatting | bytes 12288
Async XLA Ops:
  54.8 0.7 %copy-start.2 = (f32[4,2]{1,0:T(4,128)S(1)}, f32[4,2]{1,0:T(4,128)}, u32[]{:S(2)}) copy-start(f32[4,2]{1,0:T(4,128)} %get-tuple-element.15) | copy-start | bytes 100
  56.1 1.4 %copy-start.1 = (f32[2,2,3,8,16]{4,3,2,1,0:T(8,128)S(1)}, f32[2,2,3,8,16]{4,3,2,1,0:T(8,128)}, u32[]{:S(2)}) copy-start(f32[2,2,3,8,16]{4,3,2,1,0:T(8,128)} %get-tuple-element.9) | copy-start | bytes 18436
  57.5 0.8 %copy-start = (f32[2,2,3,8,16]{4,3,2,1,0:T(8,128)S(1)}, f32[2,2,3,8,16]{4,3,2,1,0:T(8,128)}, u32[]{:S(2)}) copy-start(f32[2,2,3,8,16]{4,3,2,1,0:T(8,128)} %get-tuple-element.10) | copy-start | bytes 18436

commit v2 on v1

--- a/solution.py
+++ b/solution.py
@@ -25,8 +25,8 @@
 
 def kernel(
     axes, shape, o_in, v_in, occ_in, o_out, v_out, f_out, h_out,
-    ostate, vstate, near, osend, orecv, fsend, frecv, kbuf, tally, stretch,
-    o_send_sem, o_recv_sem, f_send_sem, f_recv_sem, k_send_sem, k_recv_sem,
+    ostate, vstate, near, osend, orecv, oedge, oedges, fsend, frecv, fedge, fedges, tally, history,
+    o_send_sem, o_recv_sem, f_send_sem, f_recv_sem,
 ):
     gx, gy, gz = axes
     nx, ny, nz, slots = shape
@@ -37,9 +37,14 @@
     me = [lax.axis_index(a) for a in ("gx", "gy", "gz")]
     my_id = (me[0] * gy + me[1]) * gz + me[2]
 
-    def device(j):
-        d = lax.rem(my_id + j, devices)
-        return (d // (gy * gz), lax.rem(d // gz, gy), lax.rem(d, gz))
+    turned = [[lax.rem(me[i] + j, n) for j in range(n)] for i, n in enumerate(axes)]
+
+    def device(d):
+        return tuple(turned[i][d[i] % axes[i]] for i in range(3))
+
+    def id_of(d):
+        at = device(d)
+        return (at[0] * gy + at[1]) * gz + at[2]
 
     def canonical(size, off):
         return 0 if size == 1 else off % 2 if size == 2 else off
@@ -57,34 +62,40 @@
         (a, b, c) for a in xs for b in offsets_of(gy) for c in offsets_of(gz) if (a, b, c) != (0, 0, 0)
     ]
     slot_of = {d: i for i, d in enumerate(partners)}
+    met = {tuple(o % n for o, n in zip(d, axes)) for d in partners}
+    far = [
+        (a, b, c) for a in range(gx) for b in range(gy) for c in range(gz)
+        if (a, b, c) not in met and (a, b, c) != (0, 0, 0)
+    ]
+    level_of = [i for i, d in enumerate(partners) if d[2] == 0]
+    level_slot = {partners[i]: j for j, i in enumerate(level_of)}
 
     def layers_of(b):
         return sorted({yl for off, yl in py_of if off == b})
 
-    def halo_copies(src, dst, send_sem, recv_sem):
+    def copies_of(send, recv, edge, edge_at, send_sem, recv_sem, with_far):
         copies = []
-        for i, (a, b, c) in enumerate(partners):
-            to = (
-                lax.rem(me[0] - a + gx, gx), lax.rem(me[1] - b + gy, gy), lax.rem(me[2] - c + gz, gz),
+        for i, d in enumerate(far if with_far else []):
+            copies.append((edge.at[0, pl.ds(0, 1)], edge_at(d, 1), len(partners) + i, d))
+        for i, d in reversed([*enumerate(partners)]):
+            need = layers_of(d[1])
+            where = pl.ds(need[0], len(need))
+            if d[2] == 0:
+                copies.append((send.at[where], recv.at[level_slot[d], where], i, d))
+            else:
+                copies.append((edge.at[0 if d[2] == 1 else 1, where], edge_at(d, len(need)), i, d))
+        return [
+            pltpu.make_async_remote_copy(
+                src_ref=src, dst_ref=dst, send_sem=send_sem.at[i], recv_sem=recv_sem.at[i],
+                device_id=device(tuple(-x for x in d)), device_id_type=MESH,
             )
-            need = layers_of(b)
-            where = pl.ds(need[0], need[-1] - need[0] + 1)
-            copies.append(
-                pltpu.make_async_remote_copy(
-                    src_ref=src.at[where], dst_ref=dst.at[i, where],
-                    send_sem=send_sem.at[i], recv_sem=recv_sem.at[i],
-                    device_id=to, device_id_type=MESH,
-                )
-            )
-        return copies
+            for src, dst, i, d in copies
+        ]
 
     barrier = pltpu.get_barrier_semaphore()
 
-    def greet(j, _):
-        pl.semaphore_signal(barrier, inc=1, device_id=device(j), device_id_type=MESH)
-        return 0
-
-    lax.fori_loop(1, devices, greet, 0)
+    for d in far + partners:
+        pl.semaphore_signal(barrier, inc=1, device_id=device(d), device_id_type=MESH)
 
     lane = lax.broadcasted_iota(jnp.int32, (nz, lanes), 1)
     level = lax.broadcasted_iota(jnp.int32, (nz, lanes), 0)
@@ -112,39 +123,58 @@
                 r = c * nx + x
                 osend[y, 0, r : r + 1] = jnp.where(w > 0.5, o_rows[i : i + 1], FAR)
                 osend[y, 1, r : r + 1] = v_rows[i : i + 1] * w
-    tally[...] = jnp.sum(w_rows, axis=0, keepdims=True)
+    tally[...] = jnp.broadcast_to(jnp.sum(w_rows, keepdims=True), (1, lanes))
+
+    tile_lane = lax.broadcasted_iota(jnp.int32, (tile, lanes), 1)
+    tile_row = lax.broadcasted_iota(jnp.int32, (tile, lanes), 0)
+    ends = [lax.rem(tile_lane, slots), lax.rem(tile_lane, slots) + (lanes - slots)]
+    back = tile_row * slots + lax.rem(tile_lane, slots)
+
+    def packed(block, side):
+        taken = jnp.take_along_axis(block, ends[side], axis=1, mode="promise_in_bounds")
+        return jnp.sum(jnp.where(tile_lane // slots == tile_row, taken, 0.0), axis=0, keepdims=True)
+
+    def unpacked(row):
+        wide = jnp.broadcast_to(row, (tile, lanes))
+        return jnp.take_along_axis(wide, back, axis=1, mode="promise_in_bounds")
+
+    for side in range(2):
+        for y in range(ny):
+            for q in range(2):
+                oedge[side, y, q] = packed(osend[y, q], side)
 
     pl.semaphore_wait(barrier, devices - 1)
-    first = halo_copies(osend, orecv, o_send_sem, o_recv_sem)
+    first = copies_of(
+        osend, orecv, oedge, lambda d, n: oedges.at[slot_of[d], pl.ds(0, n)], o_send_sem, o_recv_sem, False
+    )
     for copy in first:
         copy.start()
     for copy in first:
         copy.wait()
 
-    edge_lane = lax.broadcasted_iota(jnp.int32, (tile, lanes), 1)
-
-    def columns(own, received):
+    edge_lane = tile_lane
+
+    def columns(own, level_block, edge_row):
         found = {}
         for xi, a in enumerate(xs):
             for py, (b, yl) in enumerate(py_of):
-                def block(c):
-                    d = (a, b, canonical(gz, c))
-                    return own(yl) if d == (0, 0, 0) else received(slot_of[d], yl)
-
-                mid = block(0)
+                mid = own(yl) if (a, b) == (0, 0) else level_block(level_slot[a, b, 0], yl)
                 found[xi, py, 1] = mid
-                low = jnp.where(edge_lane >= lanes - slots, block(-1), mid)
+                at = layers_of(b).index(yl)
+                below, above = (unpacked(edge_row((a, b, c), at)) for c in (-1, 1))
+                low = jnp.where(edge_lane >= lanes - slots, below, mid)
                 found[xi, py, 0] = pltpu.roll(low, slots, 1)
-                high = jnp.where(edge_lane < slots, block(1), mid)
+                high = jnp.where(edge_lane < slots, above, mid)
                 found[xi, py, 2] = pltpu.roll(high, lanes - slots, 1)
         return found
 
     for q, state in enumerate((ostate, vstate)):
-        found = columns(lambda yl: osend[yl, q], lambda s, yl: orecv[s, yl, q])
+        found = columns(
+            lambda yl: osend[yl, q], lambda s, yl: orecv[s, yl, q], lambda d, at: oedges[slot_of[d], at, q]
+        )
         for (xi, py, dz), value in found.items():
             state[xi, py, dz] = value
 
-    row_id = lax.broadcasted_iota(jnp.int32, (2 * 8, lanes), 0)
     lane_id = lax.broadcasted_iota(jnp.int32, (slots, lanes), 1)
     slot_id = lax.broadcasted_iota(jnp.int32, (slots, lanes), 0)
     pick = (lane_id // slots) * slots + slot_id
@@ -175,7 +205,8 @@
 
     def step(k, _):
         p = lax.rem(k, 2)
-        lax.fori_loop(0, ny + 2, nearby, 0)
+        for py in range(ny + 2):
+            nearby(py, 0)
 
         energy_rows = jnp.zeros((1, lanes), jnp.float32)
         for x in range(nx):
@@ -218,35 +249,26 @@
 
         kinetic = jnp.zeros((tile, lanes), jnp.float32)
         for y in range(ny):
-            v = vstate[0, y + 1, 1] + half * fsend[p, y]
+            v = vstate[0, y + 1, 1] + half * jnp.where(tile_row < 3 * nx, fsend[p, y], 0.0)
             kinetic = kinetic + v * v
-        kinetic = 0.5 * jnp.sum(kinetic, axis=0, keepdims=True)
-        kbuf[p, my_id, 0:1] = jnp.where(k == 0, tally[...], kinetic)
-        kbuf[p, my_id, 1:2] = 0.5 * energy_rows
-
-        def k_copy(j):
-            return pltpu.make_async_remote_copy(
-                src_ref=kbuf.at[p, my_id], dst_ref=kbuf.at[p, my_id],
-                send_sem=k_send_sem.at[j - 1], recv_sem=k_recv_sem.at[p, j - 1],
-                device_id=device(j), device_id_type=MESH,
-            )
-
-        def start(j, _):
-            k_copy(j).start()
-            return 0
-
-        def finish(j, _):
-            k_copy(j).wait()
-            return 0
-
-        halo = halo_copies(fsend.at[p], frecv.at[p], f_send_sem, f_recv_sem.at[p])
-
-        @pl.when(k < STEPS)
-        def _():
-            for copy in halo:
-                copy.start()
-
-        lax.fori_loop(1, devices, start, 0)
+        kinetic = 0.5 * jnp.sum(kinetic, keepdims=True)
+        kinetic = jnp.where(k == 0, tally[...], jnp.broadcast_to(kinetic, (1, lanes)))
+        potential = jnp.broadcast_to(0.5 * jnp.sum(energy_rows, keepdims=True), (1, lanes))
+        numbers = jnp.where(lane[:1] < (tile - 1) * slots, kinetic, potential)
+        fedges[p, my_id, 0] = numbers
+        for y in range(ny):
+            fsend[p, y, tile - 2 : tile - 1] = kinetic
+            fsend[p, y, tile - 1 : tile] = potential
+        for side in range(2):
+            for y in range(ny):
+                fedge[p, side, y] = packed(fsend[p, y], side)
+
+        halo = copies_of(
+            fsend.at[p], frecv.at[p], fedge.at[p], lambda d, n: fedges.at[p, my_id, pl.ds(0, n)],
+            f_send_sem, f_recv_sem.at[p], True,
+        )
+        for copy in halo:
+            copy.start()
 
         @pl.when(k == STEPS)
         def _():
@@ -254,38 +276,38 @@
                 out_planes(ostate[0, y + 1, 1], o_out, y, True)
                 out_planes(fsend[p, y], f_out, y, False)
 
-        lax.fori_loop(1, devices, finish, 0)
+        for copy in halo:
+            copy.wait()
+
+        for d in partners:
+            if d[2] == 0:
+                block = frecv[p, level_slot[d], layers_of(d[1])[0]]
+                fedges[p, id_of(d), 0] = jnp.where(
+                    lane[:1] < (tile - 1) * slots, block[tile - 2 : tile - 1], block[tile - 1 : tile]
+                )
+        parts = [fedges[p, d, 0] for d in range(devices)]
+        while len(parts) > 1:
+            parts = [sum(parts[i + 1 : i + 2], parts[i]) for i in range(0, len(parts), 2)]
+        at = (tile - 2) * slots
+        vigor = jnp.broadcast_to(parts[0][:, at : at + 1], (1, lanes))
+        potential = jnp.broadcast_to(parts[0][:, lanes - 1 :], (1, lanes))
+        count = jnp.where(k == 0, vigor, tally[...])
+        tally[...] = count
+        warmth = 2.0 * vigor / (3.0 * count)
+        lam = jnp.where(k == 0, 1.0, jnp.sqrt(1.0 + BATH_STRENGTH * (GOAL_WARMTH / warmth - 1.0)))
+        which = lax.broadcasted_iota(jnp.int32, (2, lanes), 1)
+        record = jnp.concatenate([potential, lam * lam * vigor], axis=0) / slot_total
+        history[...] = jnp.where(which == k - 1, record, history[...])
+        before = jnp.where(k > 0, half, 0.0)
 
         @pl.when(k < STEPS)
         def _():
-            for copy in halo:
-                copy.wait()
-
-        everyone = jnp.sum(kbuf[p], axis=0)
-        totals = jnp.sum(everyone, axis=1, keepdims=True)
-        vigor, potential = totals[0:1], totals[1:2]
-
-        @pl.when(k == 0)
-        def _():
-            tally[...] = jnp.broadcast_to(vigor, (1, lanes))
-            stretch[...] = jnp.ones_like(stretch)
-
-        @pl.when(k > 0)
-        def _():
-            warmth = 2.0 * jnp.broadcast_to(vigor, (1, lanes)) / (3.0 * tally[...])
-            lam = jnp.sqrt(1.0 + BATH_STRENGTH * (GOAL_WARMTH / warmth - 1.0))
-            stretch[...] = lam
-            which = lax.broadcasted_iota(jnp.int32, (1, lanes), 1)
-            record = jnp.where(which == 0, potential, lam * lam * vigor) / slot_total
-            h_out[pl.ds(k - 1, 1), :] = record[:, :2]
-
-        lam = stretch[...]
-        before = jnp.where(k > 0, half, 0.0)
-
-        @pl.when(k < STEPS)
-        def _():
-            found = columns(lambda yl: fsend[p, yl], lambda s, yl: frecv[p, s, yl])
+            found = columns(
+                lambda yl: fsend[p, yl], lambda s, yl: frecv[p, s, yl],
+                lambda d, at: fedges[p, id_of(d), at],
+            )
             for (xi, py, dz), f in found.items():
+                f = jnp.where(tile_row < 3 * nx, f, 0.0)
                 v = (vstate[xi, py, dz] + before * f) * lam
                 v = v + half * f
                 vstate[xi, py, dz] = v
@@ -296,9 +318,11 @@
             for y in range(ny):
                 v = (vstate[0, y + 1, 1] + half * fsend[p, y]) * lam
                 out_planes(v, v_out, y, False)
+            h_out[...] = history[:, :STEPS]
 
         return 0
 
+    history[...] = jnp.zeros_like(history)
     lax.fori_loop(0, STEPS + 1, step, 0)
 
 
@@ -306,9 +330,11 @@
     gx, gy, gz = axes
     nx, ny, nz, slots = occupied.shape
     lanes = nz * slots
-    tile = -(-3 * nx // 8) * 8
+    tile = lanes // slots
+    assert gz > 2 and tile >= 3 * nx + 2
     nxo, nyo, nzo = (len(offsets_of(s)) for s in axes)
     halo = nxo * nyo * nzo - 1
+    level = nxo * nyo - 1
     devices = gx * gy * gz
     f32 = jnp.float32
     plane = jax.ShapeDtypeStruct((nx, ny, 3, nz, slots), f32)
@@ -317,7 +343,7 @@
     o, v, f, h = pl.pallas_call(
         functools.partial(kernel, axes, (nx, ny, nz, slots)),
         name="verlet",
-        out_shape=[plane, plane, plane, jax.ShapeDtypeStruct((STEPS, 2), f32)],
+        out_shape=[plane, plane, plane, jax.ShapeDtypeStruct((2, STEPS), f32)],
         in_specs=[vmem] * 3,
         out_specs=[vmem] * 4,
         scratch_shapes=[
@@ -325,16 +351,17 @@
             pltpu.VMEM((nxo, ny + 2, 3, tile, lanes), f32),
             pltpu.VMEM((nx + 2, ny + 2, 3, 3, slots, lanes), f32),
             pltpu.VMEM((ny, 2, tile, lanes), f32),
-            pltpu.VMEM((halo, ny, 2, tile, lanes), f32),
+            pltpu.VMEM((max(level, 1), ny, 2, tile, lanes), f32),
+            pltpu.VMEM((2, ny, 2, 1, lanes), f32),
+            pltpu.VMEM((halo, ny, 2, 1, lanes), f32),
             pltpu.VMEM((2, ny, tile, lanes), f32),
-            pltpu.VMEM((2, halo, ny, tile, lanes), f32),
-            pltpu.VMEM((2, devices, 2, lanes), f32),
+            pltpu.VMEM((2, max(level, 1), ny, tile, lanes), f32),
+            pltpu.VMEM((2, 2, ny, 1, lanes), f32),
+            pltpu.VMEM((2, devices, ny, 1, lanes), f32),
             pltpu.VMEM((1, lanes), f32),
-            pltpu.VMEM((1, lanes), f32),
+            pltpu.VMEM((2, lanes), f32),
             dma((halo,)),
             dma((halo,)),
-            dma((halo,)),
-            dma((2, halo)),
             dma((devices - 1,)),
             dma((2, devices - 1)),
         ],
@@ -345,7 +372,7 @@
         occupied,
     )
     back = (0, 1, 3, 4, 2)
-    return (jnp.transpose(o, back), jnp.transpose(v, back), jnp.transpose(f, back), h)
+    return (jnp.transpose(o, back), jnp.transpose(v, back), jnp.transpose(f, back), h.T)
 
 
 def solution(mesh):

time: 59.3 us -> 50.7 us (0.85)
  Pallas kernels: 54.1 us -> 46.4 us
  local copies, waits for them, and re-layouts: 4.16 us -> 3.44 us
    pallas_call x1, Pallas kernels: 54.1 us -> 46.4 us  [shards(): pl.pallas_call(functools.partial(kernel, axes, (nx, ny, nz, slots)), name...]
    unnamed x10, local copies, waits for them, and re-layouts: 4.16 us -> 3.44 us
where the time goes in v2:
time: 50.7 us; the launch traced here: 50.4 us
  Pallas kernels  46.4 us (92%)
  local copies, waits for them, and re-layouts  3.44 us (7%)
  between operations  0.65 us (1%)
    pallas_call x1, Pallas kernels, shards(): pl.pallas_call(functools.partial(kernel, axes, (nx, ny, nz, slots)), name...  46.4 us
    unnamed x10, local copies, waits for them, and re-layouts  3.44 us

profile of v2, /device:TPU:0, one launch (start us, length us, event | category | flops | bytes accessed | tf_op | source)
XLA Modules:
  0.0 50.4 jit_solution(17922753494867917783)
XLA Ops:
  0.6 46.4 %verlet.1 = (f32[2,2,3,8,16]{4,3,2,1,0:T(8,128)}, f32[2,2,3,8,16]{4,3,2,1,0:T(8,128)}, f32[2,2,3,8,16]{4,3,2,1,0:T(8,128)}, f32[2,4]{1,0:T(2,128)}) custom-call(f32[2,2,3,8,16]{4,3,2,1,0:T(8,128)} %bitcast.6, f32[2,2,3,8,16]{4,3,2,1,0:T(8,128)} %bitcast.7, s32[2,2,8,16]{3,2,1,0:T(8,128)} %occ_in.1), custom_call_target="tpu_custom_call" | custom-call | tf_op jit(solution)/shard_map/verlet/pallas_call | solution.py:343
  47.0 0.0 copy-start.1
  47.0 1.4 %copy.11 = f32[2,2,8,16,3]{3,2,4,1,0:T(8,128)} copy(f32[2,2,8,16,3]{3,2,4,1,0:T(8,128)} %bitcast.10) | data formatting | bytes 12288
  48.4 0.0 copy-done.1
  48.4 0.0 copy-start
  48.4 0.6 %copy.12 = f32[2,2,8,16,3]{3,2,4,1,0:T(8,128)} copy(f32[2,2,8,16,3]{3,2,4,1,0:T(8,128)S(1)} %bitcast.9) | data formatting | bytes 12288
  49.1 0.2 copy-done
  49.3 0.0 copy-start.2
  49.3 0.6 %copy.13 = f32[2,2,8,16,3]{3,2,4,1,0:T(8,128)} copy(f32[2,2,8,16,3]{3,2,4,1,0:T(8,128)S(1)} %bitcast.8) | data formatting | bytes 12288
  49.9 0.0 copy-done.2
  49.9 0.6 %copy.14 = f32[4,2]{0,1:T(2,128)} copy(f32[4,2]{0,1:T(2,128)S(1)} %bitcast.11) | data formatting | bytes 64
Async XLA Ops:
  47.0 1.4 %copy-start.1 = (f32[2,2,3,8,16]{4,3,2,1,0:T(8,128)S(1)}, f32[2,2,3,8,16]{4,3,2,1,0:T(8,128)}, u32[]{:S(2)}) copy-start(f32[2,2,3,8,16]{4,3,2,1,0:T(8,128)} %get-tuple-element.9) | copy-start | bytes 18436
  48.4 0.8 %copy-start = (f32[2,2,3,8,16]{4,3,2,1,0:T(8,128)S(1)}, f32[2,2,3,8,16]{4,3,2,1,0:T(8,128)}, u32[]{:S(2)}) copy-start(f32[2,2,3,8,16]{4,3,2,1,0:T(8,128)} %get-tuple-element.10) | copy-start | bytes 18436
  49.3 0.6 %copy-start.2 = (f32[2,4]{1,0:T(2,128)S(1)}, f32[2,4]{1,0:T(2,128)}, u32[]{:S(2)}) copy-start(f32[2,4]{1,0:T(2,128)} %get-tuple-element.11) | copy-start | bytes 100

commit v3 on v2

--- a/solution.py
+++ b/solution.py
@@ -74,9 +74,9 @@
         return sorted({yl for off, yl in py_of if off == b})
 
     def copies_of(send, recv, edge, edge_at, send_sem, recv_sem, with_far):
-        copies = []
+        copies, remote = [], []
         for i, d in enumerate(far if with_far else []):
-            copies.append((edge.at[0, pl.ds(0, 1)], edge_at(d, 1), len(partners) + i, d))
+            remote.append((edge.at[0, pl.ds(0, 1)], edge_at(d, 1), len(partners) + i, d))
         for i, d in reversed([*enumerate(partners)]):
             need = layers_of(d[1])
             where = pl.ds(need[0], len(need))
@@ -84,17 +84,18 @@
                 copies.append((send.at[where], recv.at[level_slot[d], where], i, d))
             else:
                 copies.append((edge.at[0 if d[2] == 1 else 1, where], edge_at(d, len(need)), i, d))
-        return [
+        return [[
             pltpu.make_async_remote_copy(
                 src_ref=src, dst_ref=dst, send_sem=send_sem.at[i], recv_sem=recv_sem.at[i],
                 device_id=device(tuple(-x for x in d)), device_id_type=MESH,
             )
-            for src, dst, i, d in copies
-        ]
+            for src, dst, i, d in chosen
+        ] for chosen in ((copies, remote) if with_far else (copies,))]
 
     barrier = pltpu.get_barrier_semaphore()
 
-    for d in far + partners:
+    greeted = partners if max(n // 2 for n in axes) <= 3 else far + partners
+    for d in greeted:
         pl.semaphore_signal(barrier, inc=1, device_id=device(d), device_id_type=MESH)
 
     lane = lax.broadcasted_iota(jnp.int32, (nz, lanes), 1)
@@ -143,8 +144,8 @@
             for q in range(2):
                 oedge[side, y, q] = packed(osend[y, q], side)
 
-    pl.semaphore_wait(barrier, devices - 1)
-    first = copies_of(
+    pl.semaphore_wait(barrier, len(greeted))
+    (first,) = copies_of(
         osend, orecv, oedge, lambda d, n: oedges.at[slot_of[d], pl.ds(0, n)], o_send_sem, o_recv_sem, False
     )
     for copy in first:
@@ -252,8 +253,9 @@
             v = vstate[0, y + 1, 1] + half * jnp.where(tile_row < 3 * nx, fsend[p, y], 0.0)
             kinetic = kinetic + v * v
         kinetic = 0.5 * jnp.sum(kinetic, keepdims=True)
-        kinetic = jnp.where(k == 0, tally[...], jnp.broadcast_to(kinetic, (1, lanes)))
+        kinetic = jnp.broadcast_to(kinetic, (1, lanes))
         potential = jnp.broadcast_to(0.5 * jnp.sum(energy_rows, keepdims=True), (1, lanes))
+        potential = jnp.where(lax.rem(lane[:1], slots) < slots // 2, potential, tally[...])
         numbers = jnp.where(lane[:1] < (tile - 1) * slots, kinetic, potential)
         fedges[p, my_id, 0] = numbers
         for y in range(ny):
@@ -263,10 +265,15 @@
             for y in range(ny):
                 fedge[p, side, y] = packed(fsend[p, y], side)
 
-        halo = copies_of(
+        halo, distant = copies_of(
             fsend.at[p], frecv.at[p], fedge.at[p], lambda d, n: fedges.at[p, my_id, pl.ds(0, n)],
             f_send_sem, f_recv_sem.at[p], True,
         )
+        @pl.when(k > 0)
+        def _():
+            for copy in distant:
+                copy.start()
+
         for copy in halo:
             copy.start()
 
@@ -278,6 +285,11 @@
 
         for copy in halo:
             copy.wait()
+
+        @pl.when(k > 0)
+        def _():
+            for copy in distant:
+                copy.wait()
 
         for d in partners:
             if d[2] == 0:
@@ -290,9 +302,8 @@
             parts = [sum(parts[i + 1 : i + 2], parts[i]) for i in range(0, len(parts), 2)]
         at = (tile - 2) * slots
         vigor = jnp.broadcast_to(parts[0][:, at : at + 1], (1, lanes))
-        potential = jnp.broadcast_to(parts[0][:, lanes - 1 :], (1, lanes))
-        count = jnp.where(k == 0, vigor, tally[...])
-        tally[...] = count
+        potential = jnp.broadcast_to(parts[0][:, lanes - slots : lanes - slots + 1], (1, lanes))
+        count = jnp.broadcast_to(parts[0][:, lanes - 1 :], (1, lanes))
         warmth = 2.0 * vigor / (3.0 * count)
         lam = jnp.where(k == 0, 1.0, jnp.sqrt(1.0 + BATH_STRENGTH * (GOAL_WARMTH / warmth - 1.0)))
         which = lax.broadcasted_iota(jnp.int32, (2, lanes), 1)

time: 50.7 us -> 49.8 us (0.982)
  Pallas kernels: 46.4 us -> 45.4 us
    pallas_call x1, Pallas kernels: 46.4 us -> 45.4 us  [shards(): pl.pallas_call(functools.partial(kernel, axes, (nx, ny, nz, slots)), name...]
where the time goes in v3:
time: 49.8 us; the launch traced here: 49.5 us
  Pallas kernels  45.4 us (91%)
  local copies, waits for them, and re-layouts  3.44 us (7%)
  between operations  0.65 us (1%)
    pallas_call x1, Pallas kernels, shards(): pl.pallas_call(functools.partial(kernel, axes, (nx, ny, nz, slots)), name...  45.4 us
    unnamed x10, local copies, waits for them, and re-layouts  3.44 us

profile of v3, /device:TPU:0, one launch (start us, length us, event | category | flops | bytes accessed | tf_op | source)
XLA Modules:
  0.0 49.5 jit_solution(10326355019953551988)
XLA Ops:
  0.6 45.4 %verlet.1 = (f32[2,2,3,8,16]{4,3,2,1,0:T(8,128)}, f32[2,2,3,8,16]{4,3,2,1,0:T(8,128)}, f32[2,2,3,8,16]{4,3,2,1,0:T(8,128)}, f32[2,4]{1,0:T(2,128)}) custom-call(f32[2,2,3,8,16]{4,3,2,1,0:T(8,128)} %bitcast.6, f32[2,2,3,8,16]{4,3,2,1,0:T(8,128)} %bitcast.7, s32[2,2,8,16]{3,2,1,0:T(8,128)} %occ_in.1), custom_call_target="tpu_custom_call" | custom-call | tf_op jit(solution)/shard_map/verlet/pallas_call | solution.py:354
  46.1 0.0 copy-start.1
  46.1 1.4 %copy.11 = f32[2,2,8,16,3]{3,2,4,1,0:T(8,128)} copy(f32[2,2,8,16,3]{3,2,4,1,0:T(8,128)} %bitcast.10) | data formatting | bytes 12288
  47.5 0.0 copy-done.1
  47.5 0.0 copy-start
  47.5 0.6 %copy.12 = f32[2,2,8,16,3]{3,2,4,1,0:T(8,128)} copy(f32[2,2,8,16,3]{3,2,4,1,0:T(8,128)S(1)} %bitcast.9) | data formatting | bytes 12288
  48.1 0.2 copy-done
  48.3 0.0 copy-start.2
  48.3 0.6 %copy.13 = f32[2,2,8,16,3]{3,2,4,1,0:T(8,128)} copy(f32[2,2,8,16,3]{3,2,4,1,0:T(8,128)S(1)} %bitcast.8) | data formatting | bytes 12288
  48.9 0.0 copy-done.2
  49.0 0.6 %copy.14 = f32[4,2]{0,1:T(2,128)} copy(f32[4,2]{0,1:T(2,128)S(1)} %bitcast.11) | data formatting | bytes 64
Async XLA Ops:
  46.1 1.4 %copy-start.1 = (f32[2,2,3,8,16]{4,3,2,1,0:T(8,128)S(1)}, f32[2,2,3,8,16]{4,3,2,1,0:T(8,128)}, u32[]{:S(2)}) copy-start(f32[2,2,3,8,16]{4,3,2,1,0:T(8,128)} %get-tuple-element.9) | copy-start | bytes 18436
  47.5 0.8 %copy-start = (f32[2,2,3,8,16]{4,3,2,1,0:T(8,128)S(1)}, f32[2,2,3,8,16]{4,3,2,1,0:T(8,128)}, u32[]{:S(2)}) copy-start(f32[2,2,3,8,16]{4,3,2,1,0:T(8,128)} %get-tuple-element.10) | copy-start | bytes 18436
  48.3 0.6 %copy-start.2 = (f32[2,4]{1,0:T(2,128)S(1)}, f32[2,4]{1,0:T(2,128)}, u32[]{:S(2)}) copy-start(f32[2,4]{1,0:T(2,128)} %get-tuple-element.11) | copy-start | bytes 100

commit v4 on v3

--- a/solution.py
+++ b/solution.py
@@ -24,7 +24,7 @@
 
 
 def kernel(
-    axes, shape, o_in, v_in, occ_in, o_out, v_out, f_out, h_out,
+    axes, shape, o_in, v_in, occ_in, result,
     ostate, vstate, near, osend, orecv, oedge, oedges, fsend, frecv, fedge, fedges, tally, history,
     o_send_sem, o_recv_sem, f_send_sem, f_recv_sem,
 ):
@@ -190,17 +190,6 @@
                     row = jnp.broadcast_to(block[r : r + 1], (slots, lanes))
                     near[px, py, dz, c] = jnp.take_along_axis(row, pick, axis=1, mode="promise_in_bounds")
         return 0
-
-    def out_planes(block, ref, y, mask):
-        at = lax.broadcasted_iota(jnp.int32, (nz, lanes), 0) * slots + lax.rem(lane, slots)
-        for x in range(nx):
-            for c in range(3):
-                r = c * nx + x
-                row = jnp.broadcast_to(block[r : r + 1], (nz, lanes))
-                plane = jnp.take_along_axis(row, at, axis=1, mode="promise_in_bounds")[:, :slots]
-                if mask:
-                    plane = jnp.where(occ_in[x, y] > 0, plane, o_in[x, y, c])
-                ref[x, y, c] = plane
 
     half = 0.5 * TIME_STEP
 
@@ -277,12 +266,6 @@
         for copy in halo:
             copy.start()
 
-        @pl.when(k == STEPS)
-        def _():
-            for y in range(ny):
-                out_planes(ostate[0, y + 1, 1], o_out, y, True)
-                out_planes(fsend[p, y], f_out, y, False)
-
         for copy in halo:
             copy.wait()
 
@@ -328,13 +311,34 @@
         def _():
             for y in range(ny):
                 v = (vstate[0, y + 1, 1] + half * fsend[p, y]) * lam
-                out_planes(v, v_out, y, False)
-            h_out[...] = history[:, :STEPS]
+                result[y] = ostate[0, y + 1, 1]
+                result[ny + y] = v
+                result[2 * ny + y] = fsend[p, y]
+            result[3 * ny, 0:2] = history[...]
 
         return 0
 
     history[...] = jnp.zeros_like(history)
     lax.fori_loop(0, STEPS + 1, step, 0)
+
+
+def unpack(shape, result, o_in, occ_in, o_out, v_out, f_out, h_out):
+    nx, ny, nz, slots = shape
+    lanes = nz * slots
+    at = lax.broadcasted_iota(jnp.int32, (nz, lanes), 0) * slots + lax.rem(
+        lax.broadcasted_iota(jnp.int32, (nz, lanes), 1), slots
+    )
+    for i, ref in enumerate((o_out, v_out, f_out)):
+        for y in range(ny):
+            for x in range(nx):
+                for c in range(3):
+                    r = c * nx + x
+                    row = jnp.broadcast_to(result[i * ny + y, r : r + 1], (nz, lanes))
+                    plane = jnp.take_along_axis(row, at, axis=1, mode="promise_in_bounds")[:, :slots]
+                    if i == 0:
+                        plane = jnp.where(occ_in[x, y] > 0, plane, o_in[x, y, c])
+                    ref[x, y, c] = plane
+    h_out[...] = result[3 * ny, 0:2, :STEPS]
 
 
 def shards(axes, offsets, velocities, occupied):
@@ -351,12 +355,13 @@
     plane = jax.ShapeDtypeStruct((nx, ny, 3, nz, slots), f32)
     vmem = pl.BlockSpec(memory_space=pltpu.VMEM)
     dma = pltpu.SemaphoreType.DMA
-    o, v, f, h = pl.pallas_call(
+    o_planes = jnp.transpose(offsets, (0, 1, 4, 2, 3))
+    result = pl.pallas_call(
         functools.partial(kernel, axes, (nx, ny, nz, slots)),
         name="verlet",
-        out_shape=[plane, plane, plane, jax.ShapeDtypeStruct((2, STEPS), f32)],
+        out_shape=jax.ShapeDtypeStruct((3 * ny + 1, tile, lanes), f32),
         in_specs=[vmem] * 3,
-        out_specs=[vmem] * 4,
+        out_specs=vmem,
         scratch_shapes=[
             pltpu.VMEM((nxo, ny + 2, 3, tile, lanes), f32),
             pltpu.VMEM((nxo, ny + 2, 3, tile, lanes), f32),
@@ -378,10 +383,17 @@
         ],
         compiler_params=pltpu.CompilerParams(collective_id=0, has_side_effects=True),
     )(
-        jnp.transpose(offsets, (0, 1, 4, 2, 3)),
+        o_planes,
         jnp.transpose(velocities, (0, 1, 4, 2, 3)),
         occupied,
     )
+    o, v, f, h = pl.pallas_call(
+        functools.partial(unpack, (nx, ny, nz, slots)),
+        name="unpack",
+        out_shape=[plane, plane, plane, jax.ShapeDtypeStruct((2, STEPS), f32)],
+        in_specs=[vmem] * 3,
+        out_specs=[vmem] * 4,
+    )(result, o_planes, occupied)
     back = (0, 1, 3, 4, 2)
     return (jnp.transpose(o, back), jnp.transpose(v, back), jnp.transpose(f, back), h.T)
 

time: 49.8 us -> 47.7 us (0.958)
  local copies, waits for them, and re-layouts: 3.44 us -> 0 us
  Pallas kernels: 45.4 us -> 46.9 us
    unnamed x10 -> x0, local copies, waits for them, and re-layouts: 3.44 us -> none
    pallas_call x0 -> x1, Pallas kernels: none -> 1.54 us  [shards(): pl.pallas_call(functools.partial(unpack, (nx, ny, nz, slots)), name='unpa...]
where the time goes in v4:
time: 47.7 us; the launch traced here: 47.5 us
  Pallas kernels  46.9 us (98%)
  between operations  0.64 us (1%)
    pallas_call x1, Pallas kernels, shards(): pl.pallas_call(functools.partial(kernel, axes, (nx, ny, nz, slots)), name...  45.3 us
    pallas_call x1, Pallas kernels, shards(): pl.pallas_call(functools.partial(unpack, (nx, ny, nz, slots)), name='unpa...  1.54 us

profile of v4, /device:TPU:0, one launch (start us, length us, event | category | flops | bytes accessed | tf_op | source)
XLA Modules:
  0.0 47.5 jit_solution(9006597693413205957)
XLA Ops:
  0.6 45.3 %verlet.1.result = f32[7,8,128]{2,1,0:T(8,128)} custom-call(f32[2,2,3,8,16]{4,3,2,1,0:T(8,128)} %bitcast.6, f32[2,2,3,8,16]{4,3,2,1,0:T(8,128)} %bitcast.8, s32[2,2,8,16]{3,2,1,0:T(8,128)} %occ_in.3), custom_call_target="tpu_custom_call" | custom-call | tf_op jit(solution)/shard_map/verlet/pallas_call | solution.py:359
  46.0 1.5 %unpack.1 = (f32[2,2,3,8,16]{4,3,2,1,0:T(8,128)}, f32[2,2,3,8,16]{4,3,2,1,0:T(8,128)}, f32[2,2,3,8,16]{4,3,2,1,0:T(8,128)}, f32[2,4]{1,0:T(2,128)}) custom-call(f32[7,8,128]{2,1,0:T(8,128)} %verlet.1.result, f32[2,2,3,8,16]{4,3,2,1,0:T(8,128)} %bitcast.7, s32[2,2,8,16]{3,2,1,0:T(8,128)} %occ_in.3), custom_call_target="tpu_custom_call" | custom-call | tf_op jit(solution)/shard_map/unpack/pallas_call | solution.py:390

commit v5 on v4

--- a/solution.py
+++ b/solution.py
@@ -184,10 +184,9 @@
     def nearby(py, _):
         for px, (a, xl) in enumerate(px_of):
             for dz in range(3):
-                block = ostate[xs.index(a), py, dz]
                 for c in range(3):
                     r = c * nx + xl
-                    row = jnp.broadcast_to(block[r : r + 1], (slots, lanes))
+                    row = jnp.broadcast_to(ostate[xs.index(a), py, dz, r : r + 1], (slots, lanes))
                     near[px, py, dz, c] = jnp.take_along_axis(row, pick, axis=1, mode="promise_in_bounds")
         return 0
 
@@ -205,7 +204,7 @@
                 mine = [block[c * nx + x : c * nx + x + 1] for c in range(3)]
                 occupied = mine[0] < 0.5 * FAR
                 force = [jnp.zeros((slots, lanes), jnp.float32) for _ in range(3)]
-                energy = jnp.zeros((slots, lanes), jnp.float32)
+                bonds, reach, pairs = (jnp.zeros((slots, lanes), jnp.float32) for _ in range(3))
                 for dx in (-1, 0, 1):
                     for dy in (-1, 0, 1):
                         for dz in (-1, 0, 1):
@@ -218,20 +217,20 @@
                             if shift == (0, 0, 0):
                                 squared = jnp.where(itself, FAR, squared)
                             inside = squared < CUTOFF * CUTOFF
-                            inv = lax.rsqrt(squared)
+                            inv = jnp.where(inside, lax.rsqrt(squared), 0.0)
                             inv2 = inv * inv
                             inv6 = inv2 * inv2 * inv2
-                            pull = inv * (FORCE_EDGE - inv * inv6 * (48.0 * inv6 - 24.0))
-                            pull = jnp.where(inside, pull, 0.0)
+                            less = inv6 - 1.0
+                            pull = inv * (FORCE_EDGE / 24.0 - inv * inv6 * (inv6 + less))
                             for c in range(3):
                                 force[c] = force[c] + pull * apart[c]
-                            bond = inv6 * (4.0 * inv6 - 4.0) + (
-                                squared * inv * FORCE_EDGE - (ENERGY_EDGE + CUTOFF * FORCE_EDGE)
-                            )
-                            energy = energy + jnp.where(inside, bond, 0.0)
+                            bonds = bonds + inv6 * less
+                            reach = reach + squared * inv
+                            pairs = pairs + jnp.where(inside, 1.0, 0.0)
                 for c in range(3):
-                    total = jnp.sum(force[c], axis=0, keepdims=True)
+                    total = 24.0 * jnp.sum(force[c], axis=0, keepdims=True)
                     fsend[p, y, c * nx + x : c * nx + x + 1] = jnp.where(occupied, total, 0.0)
+                energy = 4.0 * bonds + FORCE_EDGE * reach - (ENERGY_EDGE + CUTOFF * FORCE_EDGE) * pairs
                 total = jnp.sum(energy, axis=0, keepdims=True)
                 return carried + jnp.where(occupied, total, 0.0)
 

time: 47.7 us -> 47.3 us (level)
  no operation moved by 1% of the time
where the time goes in v5:
time: 47.3 us; the launch traced here: 47.1 us
  Pallas kernels  46.5 us (98%)
  between operations  0.64 us (1%)
    pallas_call x1, Pallas kernels, shards(): pl.pallas_call(functools.partial(kernel, axes, (nx, ny, nz, slots)), name...  44.9 us
    pallas_call x1, Pallas kernels, shards(): pl.pallas_call(functools.partial(unpack, (nx, ny, nz, slots)), name='unpa...  1.54 us

profile of v5, /device:TPU:0, one launch (start us, length us, event | category | flops | bytes accessed | tf_op | source)
XLA Modules:
  0.0 47.1 jit_solution(4477009623951977292)
XLA Ops:
  0.6 44.9 %verlet.1.result = f32[7,8,128]{2,1,0:T(8,128)} custom-call(f32[2,2,3,8,16]{4,3,2,1,0:T(8,128)} %bitcast.6, f32[2,2,3,8,16]{4,3,2,1,0:T(8,128)} %bitcast.8, s32[2,2,8,16]{3,2,1,0:T(8,128)} %occ_in.3), custom_call_target="tpu_custom_call" | custom-call | tf_op jit(solution)/shard_map/verlet/pallas_call | solution.py:358
  45.5 1.5 %unpack.1 = (f32[2,2,3,8,16]{4,3,2,1,0:T(8,128)}, f32[2,2,3,8,16]{4,3,2,1,0:T(8,128)}, f32[2,2,3,8,16]{4,3,2,1,0:T(8,128)}, f32[2,4]{1,0:T(2,128)}) custom-call(f32[7,8,128]{2,1,0:T(8,128)} %verlet.1.result, f32[2,2,3,8,16]{4,3,2,1,0:T(8,128)} %bitcast.7, s32[2,2,8,16]{3,2,1,0:T(8,128)} %occ_in.3), custom_call_target="tpu_custom_call" | custom-call | tf_op jit(solution)/shard_map/unpack/pallas_call | solution.py:389

commit v6 on v5

--- a/solution.py
+++ b/solution.py
@@ -234,7 +234,8 @@
                 total = jnp.sum(energy, axis=0, keepdims=True)
                 return carried + jnp.where(occupied, total, 0.0)
 
-            energy_rows = lax.fori_loop(0, ny, one_row, energy_rows)
+            for y in range(ny):
+                energy_rows = one_row(y, energy_rows)
 
         kinetic = jnp.zeros((tile, lanes), jnp.float32)
         for y in range(ny):

time: 47.3 us -> 45.5 us (0.962)
  Pallas kernels: 46.5 us -> 44.6 us
    pallas_call x1, Pallas kernels: 44.9 us -> 43.1 us  [shards(): pl.pallas_call(functools.partial(kernel, axes, (nx, ny, nz, slots)), name...]
where the time goes in v6:
time: 45.5 us; the launch traced here: 45.3 us
  Pallas kernels  44.6 us (98%)
  between operations  0.64 us (1%)
    pallas_call x1, Pallas kernels, shards(): pl.pallas_call(functools.partial(kernel, axes, (nx, ny, nz, slots)), name...  43.1 us
    pallas_call x1, Pallas kernels, shards(): pl.pallas_call(functools.partial(unpack, (nx, ny, nz, slots)), name='unpa...  1.54 us

profile of v6, /device:TPU:0, one launch (start us, length us, event | category | flops | bytes accessed | tf_op | source)
XLA Modules:
  0.0 45.3 jit_solution(17853393128417813147)
XLA Ops:
  0.6 43.1 %verlet.1.result = f32[7,8,128]{2,1,0:T(8,128)} custom-call(f32[2,2,3,8,16]{4,3,2,1,0:T(8,128)} %bitcast.6, f32[2,2,3,8,16]{4,3,2,1,0:T(8,128)} %bitcast.8, s32[2,2,8,16]{3,2,1,0:T(8,128)} %occ_in.3), custom_call_target="tpu_custom_call" | custom-call | tf_op jit(solution)/shard_map/verlet/pallas_call | solution.py:359
  43.7 1.5 %unpack.1 = (f32[2,2,3,8,16]{4,3,2,1,0:T(8,128)}, f32[2,2,3,8,16]{4,3,2,1,0:T(8,128)}, f32[2,2,3,8,16]{4,3,2,1,0:T(8,128)}, f32[2,4]{1,0:T(2,128)}) custom-call(f32[7,8,128]{2,1,0:T(8,128)} %verlet.1.result, f32[2,2,3,8,16]{4,3,2,1,0:T(8,128)} %bitcast.7, s32[2,2,8,16]{3,2,1,0:T(8,128)} %occ_in.3), custom_call_target="tpu_custom_call" | custom-call | tf_op jit(solution)/shard_map/unpack/pallas_call | solution.py:390
